TPU v7x, 32 devices: a whole 2x2x4 slice. The times are simulated.
32 devices in a mesh: gz: 4 (over z), gy: 4 (over x, core), gx: 2 (over y).
Axes of the slice: x: 2, y: 2, z: 4, core: 2. Of those that a mesh axis runs over, the one named last changes fastest.
Arguments:
- start: float32 [128, 64, 256], P('gz', 'gy', 'gx'), may hold values from -21 to 21
- measured: float32 [128, 8, 1024], P(('gz', 'gy', 'gx')), may hold values from -18 to 18
- tiles: bfloat16 [8192, 8, 512], P('gy', None, 'gx'), may hold values from -0.125 to 0.125
- tile_block: int32 [4, 2, 8], replicated, may hold values from 0 to 3
- angle_row: int32 [8], replicated, may hold values from 0 to 7, each once
Outputs:
- estimate: float32 [128, 64, 256], P('gz', 'gy', 'gx')
- dual_state: float32 [3, 128, 64, 256], P(None, 'gz', 'gy', 'gx')
Inputs may be any that keep to these rules, and one draw needn't show every extreme that they name: `tile_block`: which of the 4 detector blocks of 256 columns each brick's tile covers at each angle. `angle_row`: every row of measured is named once.
All inputs are finite; a program needn't handle non-finite values.
Results may differ from a plain program's by a relative error of at most 0.0008.
Values may be sent and summed in bfloat16 or wider, within the bound.
A program may use at most 128 MiB of HBM per device.

v0:
```python
import functools
import math

import jax
import jax.numpy as jnp
from jax import lax
from jax.experimental import pallas as pl
from jax.experimental.pallas import tpu as pltpu
from jax.sharding import PartitionSpec as P

RADIUS = 8
ITERS = 2
NBLK = 4

blur_sigma = 2.5
step_size = 0.5
shrink_weight = 0.2
rho_start = 1.0
eps_norm = 1e-06

AXES = ("gz", "gy", "gx")
MESH = pl.DeviceIdType.MESH
HIGH = lax.Precision.HIGHEST
SPREAD = 2.0 * blur_sigma * blur_sigma
NORM = 1.0 / sum(math.exp(-k * k / SPREAD) for k in range(-RADIUS, RADIUS + 1))
TAPS = [NORM * math.exp(-k * k / SPREAD) for k in range(-RADIUS, RADIUS + 1)]
FACES = [(axis, side) for axis in AXES for side in (-1, 1)]
HALOS = [(dz, dy) for dz in (-1, 0, 1) for dy in (-1, 0, 1) if dz or dy]


def band(distance):
    near = jnp.abs(distance) <= RADIUS
    d = distance.astype(jnp.float32)
    return jnp.where(near, jnp.exp(-d * d / SPREAD) * NORM, 0.0)


def iota(shape, dim):
    return lax.broadcasted_iota(jnp.int32, shape, dim)


def dot(a, b, precision=None):
    return jnp.dot(a, b, preferred_element_type=jnp.float32, precision=precision)


def kernel(sizes, dims, start_ref, measured_ref, tiles_ref, table_ref, rows_ref, estimate_ref, dual_ref, *scratch):
    (raw, mats, ext, yb, flat, proj, send1, recv1, send2, arrived, misfit,
     hy_send, hz_send, hc_send, hy, hz, hc, x_send, x_recv, fy_send, fz_send, fx_send, fy, fz, fx,
     sum_send, sum_recv, field_ref, base_ref, back_ref, dual_s, dlow_s, send_sem, recv_sem, load_sem) = scratch
    CZ, CY, CX, ANG, DW, V, owned = dims
    bricks = sizes["gy"] * sizes["gx"]
    ngx = sizes["gx"]
    at = {axis: lax.axis_index(axis) for axis in AXES}
    me = at["gy"] * ngx + at["gx"]
    counter = [0]
    R = RADIUS
    cells = float(CZ * CY * CX * sizes["gz"] * bricks)

    def exists(steps):
        ok = None
        for axis, step in steps.items():
            if step == 0:
                continue
            test = at[axis] > 0 if step < 0 else at[axis] < sizes[axis] - 1
            ok = test if ok is None else jnp.logical_and(ok, test)
        return ok

    def remote(src, dst, target):
        slot = counter[0]
        counter[0] += 1
        return pltpu.make_async_remote_copy(
            src_ref=src, dst_ref=dst, send_sem=send_sem.at[slot], recv_sem=recv_sem.at[slot],
            device_id=target, device_id_type=MESH)

    def shift_send(src, dst_here, dst_there, steps):
        target = {axis: lax.rem(at[axis] + step + sizes[axis], sizes[axis]) for axis, step in steps.items() if step}
        copy = remote(src, dst_there, target)
        out_ok = exists(steps)
        in_ok = exists({axis: -step for axis, step in steps.items()})

        @pl.when(out_ok)
        def _():
            copy.start()

        @pl.when(jnp.logical_not(in_ok))
        def _():
            dst_here[...] = jnp.zeros(dst_here.shape, dst_here.dtype)

        def finish():
            @pl.when(out_ok)
            def _():
                copy.wait_send()

            @pl.when(in_ok)
            def _():
                copy.wait_recv()
        return finish

    chunks = 8
    per = V * ANG // chunks
    loads = [pltpu.make_async_copy(tiles_ref.at[pl.ds(i * per, per)], raw.at[pl.ds(i * per, per)], load_sem.at[i])
             for i in range(chunks)]
    for load in loads:
        load.start()
    group = 256 // ANG
    r, c = iota((256, 256), 0), iota((256, 256), 1)
    to_major = jnp.where((r // group == c % ANG) & (r % group == c // ANG), 1.0, 0.0).astype(jnp.bfloat16)

    def relayout():
        steps = per // 256
        for i in range(chunks):
            loads[i].wait()

            def one(n, carry):
                block = raw[pl.ds(pl.multiple_of(i * per + n * 256, 256), 256), :]
                moved = dot(to_major, block).astype(jnp.bfloat16)
                first = pl.multiple_of((i * steps + n) * group, group)
                for a in range(ANG):
                    mats[a, pl.ds(first, group), :] = moved[a * group:(a + 1) * group]
                return carry
            lax.fori_loop(0, steps, one, 0)

    def permute(block, transposed):
        n = CZ * ANG
        rr, cc = iota((n, n), 0), iota((n, n), 1)
        if transposed:
            m = (rr // ANG == cc % CZ) & (rr % ANG == cc // CZ)
        else:
            m = (rr // CZ == cc % ANG) & (rr % CZ == cc // ANG)
        return dot(jnp.where(m, 1.0, 0.0).astype(jnp.bfloat16), block)

    def halo_start(b, value):
        low = value.astype(jnp.bfloat16)
        hy_send[0] = low[CY - R:]
        hy_send[1] = low[:R]
        zl, zh = value[:, CZ - R:, :].astype(jnp.bfloat16), value[:, :R, :].astype(jnp.bfloat16)
        hz_send[0] = zl
        hz_send[1] = zh
        hc_send[0] = zl[CY - R:]
        hc_send[1] = zl[:R]
        hc_send[2] = zh[CY - R:]
        hc_send[3] = zh[:R]
        ends = []
        for side, step in ((0, 1), (1, -1)):
            ends.append(shift_send(hy_send.at[side], hy.at[b, side], hy.at[b, side], {"gy": step}))
            ends.append(shift_send(hz_send.at[side], hz.at[b, side], hz.at[b, side], {"gz": step}))
        for zs, zstep in ((0, 1), (1, -1)):
            for ys, ystep in ((0, 1), (1, -1)):
                s = zs * 2 + ys
                ends.append(shift_send(hc_send.at[s], hc.at[b, s], hc.at[b, s], {"gz": zstep, "gy": ystep}))
        ext[R:R + CY, R:R + CZ, :] = value
        return ends

    zi, zj = iota((CZ, CZ + 2 * R), 0), iota((CZ, CZ + 2 * R), 1)
    band_z = band(zj - R - zi)
    xi, xj = iota((CX, CX), 0), iota((CX, CX), 1)
    band_x = band(xi - xj)
    halo_at = jnp.where(xi < R, xi - R, xi - R + CX)
    band_halo = jnp.where(xi < 2 * R, band(halo_at - xj), 0.0)

    def halo_finish(b, ends, between=None):
        for end in ends:
            end()
        f32 = jnp.float32
        for side in (0, 1):
            y0 = 0 if side == 0 else R + CY
            z0 = 0 if side == 0 else R + CZ
            ext[y0:y0 + R, R:R + CZ, :] = hy[b, side].astype(f32)
            ext[R:R + CY, z0:z0 + R, :] = hz[b, side].astype(f32)
            for ys in (0, 1):
                yy = 0 if ys == 0 else R + CY
                ext[yy:yy + R, z0:z0 + R, :] = hc[b, side * 2 + ys].astype(f32)

        def one(y, carry):
            total = TAPS[0] * ext[y]
            for k in range(1, 2 * R + 1):
                total = total + TAPS[k] * ext[y + k]
            yb[y] = total
            return carry
        lax.fori_loop(0, CY, one, 0)
        wide = jnp.concatenate([yb[y] for y in range(CY)], axis=1)
        zb = dot(band_z, wide, HIGH)
        rows = jnp.concatenate([zb[:, y * CX:(y + 1) * CX] for y in range(CY)], axis=0)
        turned = rows.T
        x_send[0] = turned[CX - R:]
        x_send[1] = turned[:R]
        xends = [shift_send(x_send.at[side], x_recv.at[b, side], x_recv.at[b, side], {"gx": step})
                 for side, step in ((0, 1), (1, -1))]
        result = dot(rows, band_x, HIGH)
        if between is not None:
            between()
        for end in xends:
            end()
        edge = jnp.concatenate([x_recv[b, 0], x_recv[b, 1], jnp.zeros((CX - 2 * R, CY * CZ), jnp.float32)], axis=0)
        return result + dot(edge.T, band_halo, HIGH)

    def rims_start(n, value):
        fy_send[0] = value[CY - 1]
        fy_send[1] = value[0]
        fz_send[0] = value[:, CZ - 1, :]
        fz_send[1] = value[:, 0, :]
        turned = value.reshape(CY * CZ, CX).T
        fx_send[0] = turned[CX - 8:]
        fx_send[1] = turned[:8]
        ends = []
        for buf, got, axis in ((fy_send, fy, "gy"), (fz_send, fz, "gz"), (fx_send, fx, "gx")):
            for side, step in ((0, 1), (1, -1)):
                ends.append(shift_send(buf.at[side], got.at[n, side], got.at[n, side], {axis: step}))
        return ends

    shape = (CY, CZ, CX)
    iy, iz, ix = iota(shape, 0), iota(shape, 1), iota(shape, 2)

    def differences(n, value, ends):
        for end in ends:
            end()
        zeros = jnp.zeros((CX - 16, CY * CZ), jnp.float32)
        xcol = jnp.concatenate([fx[n, 0][7:8], jnp.zeros((CX - 2, CY * CZ), jnp.float32), fx[n, 1][0:1]], axis=0).T.reshape(shape)
        del zeros
        uppers = [
            jnp.where(iz == CZ - 1, fz[n, 1][:, None, :], pltpu.roll(value, CZ - 1, 1)),
            jnp.concatenate([value[1:], fy[n, 1][None]], axis=0),
            jnp.where(ix == CX - 1, xcol, pltpu.roll(value, CX - 1, 2)),
        ]
        lowers = [
            jnp.where(iz == 0, fz[n, 0][:, None, :], pltpu.roll(value, 1, 1)),
            jnp.concatenate([fy[n, 0][None], value[:-1]], axis=0),
            jnp.where(ix == 0, xcol, pltpu.roll(value, 1, 2)),
        ]
        jumps, before = [], []
        for axis, where, upper, lower, extent in zip(AXES, (iz, iy, ix), uppers, lowers, (CZ, CY, CX)):
            place = where + at[axis] * extent
            jumps.append(jnp.where(place == extent * sizes[axis] - 1, 0.0, upper - value))
            before.append(jnp.where(place == 0, 0.0, value - lower))
        return jumps, before

    def whole(scalar):
        return jnp.broadcast_to(scalar, (CZ, CX))[None]

    def soft(v, cut):
        return v - jnp.clip(v, -cut, cut)

    def sums_start(n, stage, value):
        slots = sum_send.at[n, stage]
        slots[...] = value
        copies = []
        axes_n = sizes["gz"] if stage == 0 else bricks
        for o in range(1, axes_n):
            if stage == 0:
                target = {"gz": lax.rem(at["gz"] + o, axes_n)}
            else:
                s = lax.rem(me + o, bricks)
                target = {"gy": s // ngx, "gx": lax.rem(s, ngx)}
            copy = remote(slots, sum_recv.at[n, stage, o], target)
            copy.start()
            copies.append(copy)
        return copies

    def sums_finish(n, stage, copies):
        total = sum_send[n, stage]
        for o, copy in enumerate(copies, 1):
            copy.wait()
            total = total + sum_recv[n, stage, o]
        return total

    def exchange(src_of, dst):
        copies = []
        for o in range(1, bricks):
            s = lax.rem(me + o, bricks)
            copy = remote(src_of(s), dst, {"gy": s // ngx, "gx": lax.rem(s, ngx)})
            copy.start()
            copies.append(copy)
        return copies

    value = jnp.swapaxes(start_ref[...], 0, 1)
    field_ref[...] = value
    halo_ends = halo_start(0, value)
    rim_ends = rims_start(0, value)
    relayout()
    value = field_ref[...]
    jumps, before = differences(0, value, rim_ends)
    penalty = jnp.full((1, 1), rho_start, jnp.float32)
    cutoff = shrink_weight / penalty
    smoothing, back = None, None
    for d in range(3):
        term = before[d] - jumps[d]
        cut = whole(cutoff)
        shr = soft(before[d], cut) - soft(jumps[d], cut)
        smoothing = term if smoothing is None else smoothing + term
        back = shr if back is None else back + shr
    base_ref[0] = smoothing
    base_ref[1] = jnp.zeros_like(smoothing)
    back_ref[...] = back
    sub = iota((ANG, DW), 0)
    tables = []

    for sweep in range(ITERS):
        last = sweep + 1 == ITERS
        pending = {}

        def between():
            if sweep:
                total = sums_finish(sweep - 1, 0, pending0["copies"])
                pending["copies"] = sums_start(sweep - 1, 1, total)
        pending0 = {"copies": sums_copies} if sweep else {}
        blurred = halo_finish(2 * sweep, halo_ends, between)
        flat[...] = jnp.concatenate([blurred[y * CZ:(y + 1) * CZ] for y in range(CY)], axis=1).astype(jnp.bfloat16)

        def forward(a, carry):
            proj[pl.ds(pl.multiple_of(a * CZ, CZ), CZ), :] = dot(flat[...], mats[a]).astype(jnp.bfloat16)
            return carry
        lax.fori_loop(0, ANG, forward, 0)
        send1[sweep] = permute(proj[...], True).reshape(CZ, ANG, DW).astype(jnp.bfloat16)
        copies = exchange(lambda s: send1.at[sweep, pl.ds(s * owned, owned)], recv1.at[sweep, me])
        recv1[sweep, me] = send1[sweep, pl.ds(me * owned, owned)]
        which = jnp.zeros((ANG, DET_OF(measured_ref)), jnp.int32)
        lane = iota(which.shape, 0)
        for a in range(ANG):
            which = jnp.where(lane == a, rows_ref[a], which)
        observed = jnp.zeros(measured_ref.shape, jnp.float32)
        for k in range(ANG):
            observed = jnp.where((which == k)[None], measured_ref[:, k:k + 1, :], observed)
        if sweep == 0:
            for s in range(bricks):
                t = jnp.zeros((ANG, DW), jnp.int32)
                for a in range(ANG):
                    t = jnp.where(sub == a, table_ref[s * ANG + a], t)
                tables.append(t)
        else:
            total = sums_finish(sweep - 1, 1, pending["copies"])
            primal_res = jnp.sum(total[0:1], axis=1, keepdims=True) / (3.0 * cells)
            dual_res = penalty * penalty * jnp.sum(total[1:2], axis=1, keepdims=True) / cells
            factor = jnp.sqrt(jnp.sqrt((primal_res + eps_norm) / (dual_res + eps_norm)))
            penalty = penalty * factor
            cutoff = shrink_weight / penalty
            for d in range(3):
                dual_s[d] = dual_s[d] / whole(factor)
                dlow_s[d] = dlow_s[d] / whole(factor)
            base_ref[1] = base_ref[1] / whole(factor)
        for copy in copies:
            copy.wait()
        sino = [jnp.zeros((owned, ANG, DW), jnp.float32) for _ in range(NBLK)]
        for s in range(bricks):
            got = recv1[sweep, s].astype(jnp.float32)
            for q in range(NBLK):
                sino[q] = sino[q] + jnp.where((tables[s] == q)[None], got, 0.0)
        for q in range(NBLK):
            sino[q] = sino[q] - observed[:, :, q * DW:(q + 1) * DW]
        for s in range(bricks):
            chosen = sino[0]
            for q in range(1, NBLK):
                chosen = jnp.where((tables[s] == q)[None], sino[q], chosen)
            send2[sweep, s] = chosen.astype(jnp.bfloat16)
        place = pl.ds(me * owned, owned)
        copies = exchange(lambda s: send2.at[sweep, s], arrived.at[sweep, place])
        arrived[sweep, place] = send2[sweep, me]
        for copy in copies:
            copy.wait()
        got = arrived[sweep].astype(jnp.float32).reshape(CZ * ANG, DW).astype(jnp.bfloat16)
        misfit[...] = permute(got, False).astype(jnp.bfloat16)

        part = V // 8

        def backward(n, carry):
            total = jnp.zeros((CZ, part), jnp.float32)
            for a in range(ANG):
                total = total + lax.dot_general(
                    misfit[a * CZ:(a + 1) * CZ, :], mats[a, pl.ds(pl.multiple_of(n * part, part), part), :],
                    (((1,), (1,)), ((), ())), preferred_element_type=jnp.float32)
            per_part = part // CX
            for i in range(per_part):
                estimate_rows[n * per_part + i] = total[:, i * CX:(i + 1) * CX]
            return carry
        estimate_rows = yb_rows(yb, CZ)
        lax.fori_loop(0, 8, backward, 0)
        halo_ends = halo_start(2 * sweep + 1, estimate_rows[...])
        grad = halo_finish(2 * sweep + 1, halo_ends).reshape(shape)
        value = field_ref[...] - step_size * (
            grad + whole(penalty) * (base_ref[0] + base_ref[1] - back_ref[...]))
        field_ref[...] = value
        rim_ends = rims_start(sweep + 1, value)
        if not last:
            halo_ends = halo_start(2 * sweep + 2, value)
        else:
            estimate_ref[...] = jnp.swapaxes(value, 0, 1)
        jumps, before = differences(sweep + 1, value, rim_ends)
        cut = whole(cutoff)
        primal = jnp.zeros((CZ, CX), jnp.float32)
        smoothing, back_new, back_dual = [jnp.zeros(shape, jnp.float32)] * 3
        for d in range(3):
            smoothing = smoothing + (before[d] - jumps[d])
            if sweep:
                total, low = jumps[d] + dual_s[d], before[d] + dlow_s[d]
            else:
                total, low = jumps[d], before[d]
            shr, shr_low = soft(total, cut), soft(low, cut)
            new, new_low = total - shr, low - shr_low
            dual_s[d] = new
            if not last:
                dlow_s[d] = new_low
                back_dual = back_dual + (new_low - new)
            back_new = back_new + (shr_low - shr)
            gap = jumps[d] - shr
            primal = primal + jnp.sum(gap * gap, axis=0)
        change = back_new - back_ref[...]
        dual_part = jnp.sum(change * change, axis=0)
        sums = jnp.concatenate([
            jnp.sum(primal, axis=0, keepdims=True), jnp.sum(dual_part, axis=0, keepdims=True),
            jnp.zeros((6, CX), jnp.float32)], axis=0)
        if not last:
            base_ref[0] = smoothing
            base_ref[1] = back_dual
            back_ref[...] = back_new
        sums_copies = sums_start(sweep, 0, sums)

    total = sums_finish(ITERS - 1, 0, sums_copies)
    final_copies = sums_start(ITERS - 1, 1, total)
    for d in range(3):
        dual_ref[d] = jnp.swapaxes(dual_s[d], 0, 1)
    total = sums_finish(ITERS - 1, 1, final_copies)
    primal_res = jnp.sum(total[0:1], axis=1, keepdims=True) / (3.0 * cells)
    dual_res = penalty * penalty * jnp.sum(total[1:2], axis=1, keepdims=True) / cells
    factor = jnp.sqrt(jnp.sqrt((primal_res + eps_norm) / (dual_res + eps_norm)))
    final = jnp.broadcast_to(factor, (CY, CX))[None]
    for d in range(3):
        dual_ref[d] = dual_ref[d] / final


def DET_OF(ref):
    return ref.shape[2]


def yb_rows(ref, depth):
    return ref.at[:, pl.ds(0, depth), :]


def body(sizes, start, measured, tiles, tile_block, angle_row):
    CZ, CY, CX = start.shape
    V, ANG, DW = tiles.shape
    owned = measured.shape[0]
    bricks = sizes["gy"] * sizes["gx"]
    R = RADIUS
    f32, bf16 = jnp.float32, jnp.bfloat16
    blurs, rims = 2 * ITERS, ITERS + 1
    slots = blurs * 10 + rims * 6 + ITERS * (2 * (bricks - 1) + bricks - 1 + sizes["gz"] - 1)
    vm = pltpu.VMEM
    scratch = [
        vm((V * ANG, DW), bf16), vm((ANG, V, DW), bf16), vm((CY + 2 * R, CZ + 2 * R, CX), f32),
        vm((CY, CZ + 2 * R, CX), f32), vm((CZ, V), bf16), vm((ANG * CZ, DW), bf16),
        vm((ITERS, CZ, ANG, DW), bf16), vm((ITERS, bricks, owned, ANG, DW), bf16),
        vm((ITERS, bricks, owned, ANG, DW), bf16), vm((ITERS, CZ, ANG, DW), bf16), vm((ANG * CZ, DW), bf16),
        vm((2, R, CZ, CX), bf16), vm((2, CY, R, CX), bf16), vm((4, R, R, CX), bf16),
        vm((blurs, 2, R, CZ, CX), bf16), vm((blurs, 2, CY, R, CX), bf16), vm((blurs, 4, R, R, CX), bf16),
        vm((2, R, CY * CZ), f32), vm((blurs, 2, R, CY * CZ), f32),
        vm((2, CZ, CX), f32), vm((2, CY, CX), f32), vm((2, 8, CY * CZ), f32),
        vm((rims, 2, CZ, CX), f32), vm((rims, 2, CY, CX), f32), vm((rims, 2, 8, CY * CZ), f32),
        vm((ITERS, 2, 8, CX), f32), vm((ITERS, 2, max(bricks, sizes["gz"]), 8, CX), f32),
        vm((CY, CZ, CX), f32), vm((2, CY, CZ, CX), f32), vm((CY, CZ, CX), f32),
        vm((3, CY, CZ, CX), f32), vm((3, CY, CZ, CX), f32),
        pltpu.SemaphoreType.DMA((slots,)), pltpu.SemaphoreType.DMA((slots,)), pltpu.SemaphoreType.DMA((8,)),
    ]
    vmem = pl.BlockSpec(memory_space=pltpu.VMEM)
    smem = pl.BlockSpec(memory_space=pltpu.SMEM)
    return pl.pallas_call(
        functools.partial(kernel, sizes, (CZ, CY, CX, ANG, DW, V, owned)),
        out_shape=(jax.ShapeDtypeStruct((CZ, CY, CX), f32), jax.ShapeDtypeStruct((3, CZ, CY, CX), f32)),
        in_specs=[vmem, vmem, pl.BlockSpec(memory_space=pl.ANY), smem, smem],
        out_specs=(vmem, vmem),
        scratch_shapes=scratch,
        compiler_params=pltpu.CompilerParams(has_side_effects=True, vmem_limit_bytes=60 * 1024 * 1024),
    )(start, measured, tiles.reshape(V * ANG, DW), tile_block.reshape(-1), angle_row)


def solution(mesh):
    return jax.shard_map(
        functools.partial(body, dict(mesh.shape)),
        mesh=mesh,
        in_specs=(
            P("gz", "gy", "gx"),
            P(("gz", "gy", "gx"), None, None),
            P("gy", None, "gx"),
            P(),
            P(),
        ),
        out_specs=(P("gz", "gy", "gx"), P(None, "gz", "gy", "gx")),
        check_vma=False,
    )
```

profile of v0, /device:TPU:0, one launch (start us, length us, event | category | flops | bytes accessed | tf_op | source)
XLA Modules:
  0.0 98.2 jit_solution(5647078638576405290)
XLA Ops:
  0.6 1.3 %reshape.11.table_ref = s32[64]{0:T(128)} reshape(s32[4,2,8]{2,1,0:T(2,128)} %param.8) | data formatting | bytes 512 | tf_op jit(solution)/shard_map/reshape | solution.py:470
  1.9 92.5 %shard_map.68 = (f32[32,16,128]{2,1,0:T(8,128)}, f32[3,32,16,128]{3,2,1,0:T(8,128)}) custom-call(f32[32,16,128]{2,1,0:T(8,128)} %start_ref.1, f32[4,8,1024]{2,1,0:T(8,128)} %measured_ref.1, bf16[16384,256]{1,0:T(8,128)(2,1)} %bitcast.1, s32[64]{0:T(128)} %reshape.11.table_ref, s32[8]{0:T(128)} %rows_ref.1), custom_call_target="tpu_custom_call" | custom-call | tf_op jit(solution)/shard_map/pallas_call | solution.py:463
  94.4 1.7 %copy.9 = f32[32,16,128]{2,1,0:T(8,128)} copy(f32[32,16,128]{2,1,0:T(8,128)} %get-tuple-element.4) | data formatting | bytes 524288
  96.1 2.1 %copy.10 = f32[3,32,16,128]{3,2,1,0:T(8,128)} copy(f32[3,32,16,128]{3,2,1,0:T(8,128)} %get-tuple-element.5) | data formatting | bytes 1572864
where the time goes:
time: 98.4 us; the launch traced here: 98.2 us
  Pallas kernels  92.5 us (94%)
  local copies, waits for them, and re-layouts  5.02 us (5%)
    pallas_call x1, Pallas kernels, body(): pl.pallas_call(functools.partial(kernel, sizes, (CZ, CY, CX, ANG, DW, V,...  92.5 us
    unnamed x2, local copies, waits for them, and re-layouts  3.73 us

commit v1 on v0

--- a/solution.py
+++ b/solution.py
@@ -42,10 +42,10 @@
     return jnp.dot(a, b, preferred_element_type=jnp.float32, precision=precision)
 
 
-def kernel(sizes, dims, start_ref, measured_ref, tiles_ref, table_ref, rows_ref, estimate_ref, dual_ref, *scratch):
+def kernel(sizes, dims, start_hbm, measured_hbm, tiles_ref, table_hbm, rows_hbm, estimate_hbm, dual_hbm, factor_ref, *scratch):
     (raw, mats, ext, yb, flat, proj, send1, recv1, send2, arrived, misfit,
      hy_send, hz_send, hc_send, hy, hz, hc, x_send, x_recv, fy_send, fz_send, fx_send, fy, fz, fx,
-     sum_send, sum_recv, field_ref, base_ref, back_ref, dual_s, dlow_s, send_sem, recv_sem, load_sem) = scratch
+     sum_send, sum_recv, field_ref, base_ref, back_ref, dual_s, dlow_s, start_ref, measured_ref, estimate_ref, dual_ref, table_ref, rows_ref, send_sem, recv_sem, load_sem, io_sem) = scratch
     CZ, CY, CX, ANG, DW, V, owned = dims
     bricks = sizes["gy"] * sizes["gx"]
     ngx = sizes["gx"]
@@ -99,7 +99,29 @@
     per = V * ANG // chunks
     loads = [pltpu.make_async_copy(tiles_ref.at[pl.ds(i * per, per)], raw.at[pl.ds(i * per, per)], load_sem.at[i])
              for i in range(chunks)]
+    start_load = pltpu.make_async_copy(start_hbm, start_ref, io_sem.at[0])
+    measured_load = pltpu.make_async_copy(measured_hbm, measured_ref, io_sem.at[1])
+    start_load.start()
+
+    barrier = pltpu.get_barrier_semaphore()
+    partners = 0
+    for o in range(1, bricks):
+        s = lax.rem(me + o, bricks)
+        pl.semaphore_signal(barrier, inc=1, device_id={"gy": s // ngx, "gx": lax.rem(s, ngx)}, device_id_type=MESH)
+        partners += 1
+    for o in range(1, sizes["gz"]):
+        pl.semaphore_signal(barrier, inc=1, device_id={"gz": lax.rem(at["gz"] + o, sizes["gz"])}, device_id_type=MESH)
+        partners += 1
+    corners = [{"gz": dz, "gy": dy} for dz in (-1, 1) for dy in (-1, 1)]
+    for steps in corners:
+        target = {axis: lax.rem(at[axis] + step + sizes[axis], sizes[axis]) for axis, step in steps.items()}
+        pl.semaphore_signal(barrier, inc=1, device_id=target, device_id_type=MESH)
+        partners += 1
     for load in loads:
+        load.start()
+    small_loads = [measured_load, pltpu.make_async_copy(table_hbm, table_ref, io_sem.at[4]),
+                   pltpu.make_async_copy(rows_hbm, rows_ref, io_sem.at[5])]
+    for load in small_loads:
         load.start()
     group = 256 // ANG
     r, c = iota((256, 256), 0), iota((256, 256), 1)
@@ -117,7 +139,7 @@
                 for a in range(ANG):
                     mats[a, pl.ds(first, group), :] = moved[a * group:(a + 1) * group]
                 return carry
-            lax.fori_loop(0, steps, one, 0)
+            lax.fori_loop(0, steps, one, 0, unroll=True)
 
     def permute(block, transposed):
         n = CZ * ANG
@@ -271,11 +293,15 @@
             copies.append(copy)
         return copies
 
+    start_load.wait()
     value = jnp.swapaxes(start_ref[...], 0, 1)
     field_ref[...] = value
+    pl.semaphore_wait(barrier, partners)
     halo_ends = halo_start(0, value)
     rim_ends = rims_start(0, value)
     relayout()
+    for load in small_loads:
+        load.wait()
     value = field_ref[...]
     jumps, before = differences(0, value, rim_ends)
     penalty = jnp.full((1, 1), rho_start, jnp.float32)
@@ -308,7 +334,7 @@
         def forward(a, carry):
             proj[pl.ds(pl.multiple_of(a * CZ, CZ), CZ), :] = dot(flat[...], mats[a]).astype(jnp.bfloat16)
             return carry
-        lax.fori_loop(0, ANG, forward, 0)
+        lax.fori_loop(0, ANG, forward, 0, unroll=4)
         send1[sweep] = permute(proj[...], True).reshape(CZ, ANG, DW).astype(jnp.bfloat16)
         copies = exchange(lambda s: send1.at[sweep, pl.ds(s * owned, owned)], recv1.at[sweep, me])
         recv1[sweep, me] = send1[sweep, pl.ds(me * owned, owned)]
@@ -323,7 +349,7 @@
             for s in range(bricks):
                 t = jnp.zeros((ANG, DW), jnp.int32)
                 for a in range(ANG):
-                    t = jnp.where(sub == a, table_ref[s * ANG + a], t)
+                    t = jnp.where(sub == a, table_ref[s // ngx, s % ngx, a], t)
                 tables.append(t)
         else:
             total = sums_finish(sweep - 1, 1, pending["copies"])
@@ -371,7 +397,7 @@
                 estimate_rows[n * per_part + i] = total[:, i * CX:(i + 1) * CX]
             return carry
         estimate_rows = yb_rows(yb, CZ)
-        lax.fori_loop(0, 8, backward, 0)
+        lax.fori_loop(0, 8, backward, 0, unroll=4)
         halo_ends = halo_start(2 * sweep + 1, estimate_rows[...])
         grad = halo_finish(2 * sweep + 1, halo_ends).reshape(shape)
         value = field_ref[...] - step_size * (
@@ -382,6 +408,8 @@
             halo_ends = halo_start(2 * sweep + 2, value)
         else:
             estimate_ref[...] = jnp.swapaxes(value, 0, 1)
+            estimate_out = pltpu.make_async_copy(estimate_ref, estimate_hbm, io_sem.at[2])
+            estimate_out.start()
         jumps, before = differences(sweep + 1, value, rim_ends)
         cut = whole(cutoff)
         primal = jnp.zeros((CZ, CX), jnp.float32)
@@ -404,8 +432,7 @@
         change = back_new - back_ref[...]
         dual_part = jnp.sum(change * change, axis=0)
         sums = jnp.concatenate([
-            jnp.sum(primal, axis=0, keepdims=True), jnp.sum(dual_part, axis=0, keepdims=True),
-            jnp.zeros((6, CX), jnp.float32)], axis=0)
+            jnp.sum(primal, axis=0, keepdims=True), jnp.sum(dual_part, axis=0, keepdims=True)], axis=0)
         if not last:
             base_ref[0] = smoothing
             base_ref[1] = back_dual
@@ -416,13 +443,22 @@
     final_copies = sums_start(ITERS - 1, 1, total)
     for d in range(3):
         dual_ref[d] = jnp.swapaxes(dual_s[d], 0, 1)
+    dual_out = pltpu.make_async_copy(dual_ref, dual_hbm, io_sem.at[3])
+    dual_out.start()
     total = sums_finish(ITERS - 1, 1, final_copies)
     primal_res = jnp.sum(total[0:1], axis=1, keepdims=True) / (3.0 * cells)
     dual_res = penalty * penalty * jnp.sum(total[1:2], axis=1, keepdims=True) / cells
     factor = jnp.sqrt(jnp.sqrt((primal_res + eps_norm) / (dual_res + eps_norm)))
-    final = jnp.broadcast_to(factor, (CY, CX))[None]
+    factor_ref[...] = jnp.broadcast_to(factor, factor_ref.shape)
+    estimate_out.wait()
+    dual_out.wait()
+
+
+def finish(estimate_ref, dual_ref, factor_ref, estimate_out, dual_out):
+    estimate_out[...] = estimate_ref[...]
+    factor = jnp.broadcast_to(factor_ref[0:1, :], estimate_ref.shape[1:])[None]
     for d in range(3):
-        dual_ref[d] = dual_ref[d] / final
+        dual_out[d] = dual_ref[d] / factor
 
 
 def DET_OF(ref):
@@ -453,21 +489,33 @@
         vm((2, R, CY * CZ), f32), vm((blurs, 2, R, CY * CZ), f32),
         vm((2, CZ, CX), f32), vm((2, CY, CX), f32), vm((2, 8, CY * CZ), f32),
         vm((rims, 2, CZ, CX), f32), vm((rims, 2, CY, CX), f32), vm((rims, 2, 8, CY * CZ), f32),
-        vm((ITERS, 2, 8, CX), f32), vm((ITERS, 2, max(bricks, sizes["gz"]), 8, CX), f32),
+        vm((ITERS, 2, 2, CX), f32), vm((ITERS, 2, max(bricks, sizes["gz"]), 2, CX), f32),
         vm((CY, CZ, CX), f32), vm((2, CY, CZ, CX), f32), vm((CY, CZ, CX), f32),
         vm((3, CY, CZ, CX), f32), vm((3, CY, CZ, CX), f32),
+        vm(start.shape, f32), vm(measured.shape, f32), vm(start.shape, f32), vm((3,) + start.shape, f32),
+        pltpu.SMEM(tile_block.shape, jnp.int32), pltpu.SMEM(angle_row.shape, jnp.int32),
         pltpu.SemaphoreType.DMA((slots,)), pltpu.SemaphoreType.DMA((slots,)), pltpu.SemaphoreType.DMA((8,)),
+        pltpu.SemaphoreType.DMA((6,)),
     ]
     vmem = pl.BlockSpec(memory_space=pltpu.VMEM)
-    smem = pl.BlockSpec(memory_space=pltpu.SMEM)
+    hbm = pl.BlockSpec(memory_space=pl.ANY)
+    shapes = (jax.ShapeDtypeStruct((CZ, CY, CX), f32), jax.ShapeDtypeStruct((3, CZ, CY, CX), f32))
+    estimate, dual, factor = pl.pallas_call(
+        functools.partial(kernel, sizes, (CZ, CY, CX, ANG, DW, V, owned)),
+        out_shape=shapes + (jax.ShapeDtypeStruct((8, CX), f32),),
+        in_specs=[pl.BlockSpec(memory_space=pltpu.HBM)] * 5,
+        out_specs=(hbm, hbm, vmem),
+        scratch_shapes=scratch,
+        compiler_params=pltpu.CompilerParams(
+            collective_id=0, has_side_effects=True, vmem_limit_bytes=65900000),
+    )(start, measured, tiles.reshape(V * ANG, DW), tile_block, angle_row)
     return pl.pallas_call(
-        functools.partial(kernel, sizes, (CZ, CY, CX, ANG, DW, V, owned)),
-        out_shape=(jax.ShapeDtypeStruct((CZ, CY, CX), f32), jax.ShapeDtypeStruct((3, CZ, CY, CX), f32)),
-        in_specs=[vmem, vmem, pl.BlockSpec(memory_space=pl.ANY), smem, smem],
+        finish,
+        out_shape=shapes,
+        in_specs=[vmem, vmem, vmem],
         out_specs=(vmem, vmem),
-        scratch_shapes=scratch,
-        compiler_params=pltpu.CompilerParams(has_side_effects=True, vmem_limit_bytes=60 * 1024 * 1024),
-    )(start, measured, tiles.reshape(V * ANG, DW), tile_block.reshape(-1), angle_row)
+        compiler_params=pltpu.CompilerParams(vmem_limit_bytes=65900000),
+    )(estimate, dual, factor)
 
 
 def solution(mesh):

time: 98.4 us -> 78.9 us (0.80)
  Pallas kernels: 92.5 us -> 78.1 us
  local copies, waits for them, and re-layouts: 5.02 us -> 0 us
    pallas_call x1, Pallas kernels: 92.5 us -> 76 us  [body(): pl.pallas_call(functools.partial(kernel, sizes, (CZ, CY, CX, ANG, DW, V,...]
    unnamed x2 -> x0, local copies, waits for them, and re-layouts: 3.73 us -> none
    pallas_call x0 -> x1, Pallas kernels: none -> 2.17 us  [body(): pl.pallas_call(finish, out_shape=shapes, in_specs=[vmem, vmem, vmem], out...]
    reshape x1 -> x0, local copies, waits for them, and re-layouts: 1.28 us -> none  [body(): tile_block.reshape(-1)]
where the time goes in v1:
time: 78.9 us; the launch traced here: 78.8 us
  Pallas kernels  78.1 us (99%)
    pallas_call x1, Pallas kernels, body(): pl.pallas_call(functools.partial(kernel, sizes, (CZ, CY, CX, ANG, DW, V,...  76 us
    pallas_call x1, Pallas kernels, body(): pl.pallas_call(finish, out_shape=shapes, in_specs=[vmem, vmem, vmem], out...  2.17 us

profile of v1, /device:TPU:0, one launch (start us, length us, event | category | flops | bytes accessed | tf_op | source)
XLA Modules:
  0.0 78.8 jit_solution(7743117825293699799)
XLA Ops:
  0.6 76.0 %shard_map.68 = (f32[32,16,128]{2,1,0:T(8,128)}, f32[3,32,16,128]{3,2,1,0:T(8,128)}, f32[8,128]{1,0:T(8,128)}) custom-call(f32[32,16,128]{2,1,0:T(8,128)} %start_hbm.1, f32[4,8,1024]{2,1,0:T(8,128)} %measured_hbm.1, bf16[16384,256]{1,0:T(8,128)(2,1)} %bitcast.1, s32[4,2,8]{2,1,0:T(2,128)} %table_hbm.1, s32[8]{0:T(128)} %rows_hbm.1), custom_call_target="tpu_custom_call" | custom-call | tf_op jit(solution)/shard_map/pallas_call | solution.py:503
  76.6 2.2 %shard_map.69 = (f32[32,16,128]{2,1,0:T(8,128)}, f32[3,32,16,128]{3,2,1,0:T(8,128)}) custom-call(f32[32,16,128]{2,1,0:T(8,128)} %get-tuple-element.5.estimate_ref, f32[3,32,16,128]{3,2,1,0:T(8,128)} %get-tuple-element.6.dual_ref, f32[8,128]{1,0:T(8,128)} %get-tuple-element.7.factor_ref), custom_call_target="tpu_custom_call" | custom-call | tf_op jit(solution)/shard_map/pallas_call | solution.py:512
